TPU v7x, 256 devices: a whole 4x4x8 slice. The times are simulated.
256 devices in a mesh: dp: 8 (over x, core), tensor: 32 (over z, y).
Axes of the slice: x: 4, y: 4, z: 8, core: 2. Of those that a mesh axis runs over, the one named last changes fastest.
Arguments:
- hidden: bfloat16 [6144, 4096], P('dp', 'tensor'), may hold values from -2000 to 2000
- out_embed: bfloat16 [65536, 4096], P('tensor', 'dp'), may hold values from -0.3 to 0.3
- labels: int32 [6144], P('dp'), may hold values from 0 to 65535
Outputs:
- token_loss: float32 [6144], P(('dp', 'tensor'))
- mean_loss: float32 [], replicated
All inputs are finite; a program needn't handle non-finite values.
Results may differ from a plain program's by a relative error of at most 0.0003.
Values may be sent and summed in bfloat16 or wider, within the bound.
A program may use at most 128 MiB of HBM per device.

v0:
```python
import jax
import jax.numpy as jnp
from jax import lax
from jax.sharding import Mesh
from jax.sharding import PartitionSpec as P

BLOCK = 512
TENSOR = ("tensor_0", "tensor_1")
DP = ("dp_0", "dp_1")
DP_TENSOR = ("dp_0", "dp_1", "tensor_0", "tensor_1")


def whole_of(shard, axes, dim):
    for axis in reversed(axes):
        shard = lax.all_gather(shard, axis, axis=dim, tiled=True)
    return shard


def side_by_side(arrays, axis, split_dim, concat_dim, along):
    both = jnp.concatenate(arrays, axis=along)
    filled, at, done = (
        lax.all_to_all(both, axis, split_axis=split_dim, concat_axis=concat_dim, tiled=True),
        0,
        [],
    )
    for a in arrays:
        done.append(lax.slice_in_dim(filled, at, at + a.shape[along], axis=along))
        at += a.shape[along]
    return tuple(done)


def one_axis_at_a_time(shard, axes):
    for axis in axes:
        shard = lax.psum(shard, axis)
    return shard


def combine_stats(first, second):
    peak_first, mass_first, label_first = first
    peak_second, mass_second, label_second = second
    peak_value = jnp.maximum(peak_first, peak_second)
    exp_total = mass_first * jnp.exp(peak_first - peak_value) + mass_second * jnp.exp(
        peak_second - peak_value
    )
    return (peak_value, exp_total, label_first + label_second)


def block_stats(logits, first_row, labels):
    peak_value = jnp.max(logits, axis=0)
    exp_total = jnp.sum(jnp.exp(logits - peak_value[None, :]), axis=0)
    row_ids = first_row + lax.broadcasted_iota(jnp.int32, logits.shape, 0)
    label_logit = jnp.sum(
        jnp.where(row_ids == labels[None, :], logits, jnp.zeros_like(logits)), axis=0
    )
    return (peak_value, exp_total, label_logit)


def body(hidden, out_embed, labels):
    full_hidden = whole_of(hidden, TENSOR, 1)
    token_count = full_hidden.shape[0]
    vocab_rows = out_embed.shape[0]
    vocab_offset = lax.axis_index(TENSOR) * vocab_rows
    block_count = vocab_rows // BLOCK
    all_logits = lax.dot_general(
        lax.all_gather(out_embed, DP, axis=1, tiled=True),
        full_hidden,
        (((1,), (1,)), ((), ())),
        preferred_element_type=jnp.float32,
    )
    running_stats = None
    for block_index in range(block_count):
        stats = block_stats(
            all_logits[block_index * BLOCK : (block_index + 1) * BLOCK],
            vocab_offset + block_index * BLOCK,
            labels,
        )
        running_stats = stats if running_stats is None else combine_stats(running_stats, stats)
    groups = lax.axis_size(TENSOR)
    share = token_count // groups
    peak_all, mass_all, label_all = running_stats
    peaks, masses, picked = side_by_side(
        (
            peak_all.reshape(groups, share),
            mass_all.reshape(groups, share),
            label_all.reshape(groups, share),
        ),
        TENSOR,
        0,
        0,
        1,
    )
    peak_value = jnp.max(peaks, axis=0)
    exp_total = jnp.sum(masses * jnp.exp(peaks - peak_value[None, :]), axis=0)
    label_logit = jnp.sum(picked, axis=0)
    token_loss = jnp.log(exp_total) + peak_value - label_logit
    loss_sum = one_axis_at_a_time(jnp.sum(token_loss), DP_TENSOR)
    mean_loss = loss_sum / (share * lax.axis_size(DP) * groups)
    return (token_loss, mean_loss)


def solution(mesh):
    finer = Mesh(mesh.devices.reshape(4, 2, 8, 4), ("dp_0", "dp_1", "tensor_0", "tensor_1"))
    return jax.shard_map(
        body,
        mesh=finer,
        in_specs=(P(DP, TENSOR), P(TENSOR, DP), P(DP)),
        out_specs=(P(DP_TENSOR), P()),
        check_vma=False,
    )
```

profile of v0, /device:TPU:1, one launch (start us, length us, event | category | flops | bytes accessed | tf_op | source)
XLA Modules:
  0.0 278.0 jit_solution(3417769360817746753)
XLA Ops:
  7.2 0.0 all-gather.5.cloned.1.call-start
  7.2 18.9 %all_gather.10 = bf16[768,512]{1,0:T(8,128)(2,1)} all-gather(bf16[768,128]{1,0:T(8,128)(2,1)} %param.3), channel_id=1, replica_groups=mesh['dp_0'=4,'dp_1'=2,'tensor_0'=8,'tensor_1'=4] {'tensor_1'}, dimensions={1}, use_global_device_ids=true | all-gather | bytes 983040 | tf_op jit(solution)/shard_map/all_gather | solution.py:15
  26.1 0.0 all-gather.5.cloned.1.call-update
  26.1 0.0 all-gather.3.cloned.1.call-start
  26.2 0.7 all-gather.3.cloned.1.call-update
  26.9 75.9 %all-gather.5.cloned.1.call-done = bf16[768,4096]{1,0:T(8,128)(2,1)} async-done(((bf16[768,512]{1,0:T(8,128)(2,1)}), bf16[768,4096]{1,0:T(8,128)(2,1)}) %all-gather.5.cloned.1.call-update) | async-done | bytes 6291472 | tf_op jit(solution)/shard_map/all_gather | solution.py:15
  102.8 88.5 %all-gather.3.cloned.1.call-done = bf16[2048,4096]{1,0:T(8,128)(2,1)} async-done(((bf16[2048,512]{1,0:T(8,128)(2,1)}), bf16[2048,4096]{1,0:T(8,128)(2,1)}) %all-gather.3.cloned.1.call-update) | async-done | bytes 16777232 | tf_op jit(solution)/shard_map/all_gather | solution.py:65
  191.3 18.3 %fusion.3 = f32[2048,768]{1,0:T(8,128)S(1)} fusion(bf16[2048,4096]{1,0:T(8,128)(2,1)} %all-gather.3.cloned.1.call-done, bf16[768,4096]{1,0:T(8,128)(2,1)} %all-gather.5.cloned.1.call-done), kind=kOutput, calls=%fused_computation.26 | convolution fusion | flops 12884901888 | bytes 29360128 | tf_op jit(solution)/shard_map/dot_general | solution.py:64
  209.6 0.0 copy-start
  209.6 0.0 copy-start.1
  209.6 0.3 slice_reduce_fusion.1
  209.9 2.3 copy-done
  212.3 0.1 reduce_max.60
  212.3 0.1 reduce_max.58
  212.4 0.1 reduce_max.54
  212.5 0.1 reduce_max.56
  212.6 0.0 copy-done.1
  212.6 3.7 %exponential_reduce_fusion.3 = (f32[768]{0:T(1024)S(1)}, f32[768]{0:T(1024)S(1)}, f32[768]{0:T(1024)S(1)}, f32[768]{0:T(1024)S(1)}, f32[768]{0:T(1024)S(1)}, /*i...) fusion(f32[2048,768]{1,0:T(8,128)} %copy-done, f32[768]{0:T(1024)S(1)} %get-tuple-element.17, ...), kind=kLoop, calls=%fused_computation.7 | loop fusion | flops 7858176 | bytes 6339584 | tf_op jit(solution)/shard_map/reduce_sum | solution.py:50
  216.3 0.1 add.98
  216.4 0.1 reduce_sum.114
  216.5 0.1 reduce_sum.112
  216.6 0.1 reduce_sum.110
  216.6 0.1 reduce_sum.108
  216.8 0.1 pad_maximum_fusion
  216.9 18.0 %all_to_all.12 = f32[32,1,72]{2,1,0:T(1,128)S(1)} all-to-all(f32[32,1,72]{2,1,0:T(1,128)S(1)} %bitcast.8), channel_id=1, replica_groups=mesh['dp_0'=4,'dp_1'=2,'tensor_0'=8,'tensor_1'=4] {'tensor_0','tensor_1'}, dimensions={0} | all-to-all | bytes 18432 | tf_op jit(solution)/shard_map/all_to_all | solution.py:22
  234.9 0.1 fusion
  235.0 1.1 fusion.1
  236.1 8.1 %psum.28 = f32[]{:T(128)} all-reduce(f32[]{:T(128)} %get-tuple-element.20), channel_id=1, replica_groups=mesh['dp_0'=4,'dp_1'=2,'tensor_0'=8,'tensor_1'=4] {'dp_0'}, use_global_device_ids=true, to_apply=%region_16.17 | all-reduce | flops 1 | bytes 8 | tf_op jit(solution)/shard_map/psum | solution.py:34
  244.1 6.1 %psum.29 = f32[]{:T(128)} all-reduce(f32[]{:T(128)} %psum.28), channel_id=1, replica_groups=mesh['dp_0'=4,'dp_1'=2,'tensor_0'=8,'tensor_1'=4] {'dp_1'}, use_global_device_ids=true, to_apply=%region_17.18 | all-reduce | flops 1 | bytes 8 | tf_op jit(solution)/shard_map/psum | solution.py:34
  250.2 11.7 %psum.30 = f32[]{:T(128)} all-reduce(f32[]{:T(128)} %psum.29), channel_id=1, replica_groups=mesh['dp_0'=4,'dp_1'=2,'tensor_0'=8,'tensor_1'=4] {'tensor_0'}, use_global_device_ids=true, to_apply=%region_18.19 | all-reduce | flops 1 | bytes 8 | tf_op jit(solution)/shard_map/psum | solution.py:34
  261.9 7.5 %psum.31 = f32[]{:T(128)} all-reduce(f32[]{:T(128)} %psum.30), channel_id=1, replica_groups=mesh['dp_0'=4,'dp_1'=2,'tensor_0'=8,'tensor_1'=4] {'tensor_1'}, use_global_device_ids=true, to_apply=%region_19.20 | all-reduce | flops 1 | bytes 8 | tf_op jit(solution)/shard_map/psum | solution.py:34
  (6 shorter events, 0.1 us)
Async XLA Ops:
  7.2 95.6 %all-gather.5.cloned.1.call-start = ((), (), s32[]{:S(2)}) async-start(), calls=%async_computation.2 | async-start | bytes 7077888 | tf_op jit(solution)/shard_map/all_gather | solution.py:15
  26.1 165.2 %all-gather.3.cloned.1.call-start = ((), (), s32[]{:S(2)}) async-start(), calls=%async_computation.1 | async-start | bytes 18874368 | tf_op jit(solution)/shard_map/all_gather | solution.py:65
  209.6 2.7 copy-start
  209.6 3.0 %copy-start.1 = (s32[768]{0:T(1024)S(1)}, s32[768]{0:T(1024)}, u32[]{:S(2)}) copy-start(s32[768]{0:T(1024)} %param.5) | copy-start | bytes 9220
Sparse Core Ops, SparseCore 0:
  26.2 76.5 all-gather.4
  104.6 86.5 all-gather.2
where the time goes:
time: 282 us; the launch traced here: 278 us
  waiting for transfers between devices  165 us (59%)
  blocking collectives  70.2 us (25%)
  matrix products  18.3 us (6%)
  between operations  16 us (6%)
  other arithmetic  5.37 us (2%)
  local copies, waits for them, and re-layouts  3.03 us (1%)
    all_gather x1, waiting for transfers between devices, body(): lax.all_gather(out_embed, DP, axis=1, tiled=True)  88.5 us
    all_gather x1, waiting for transfers between devices, whole_of(): shard = lax.all_gather(shard, axis, axis=dim, tiled=True)  75.9 us
    psum x4, blocking collectives, one_axis_at_a_time(): shard = lax.psum(shard, axis)  33.3 us
    all_gather x1, blocking collectives, whole_of(): shard = lax.all_gather(shard, axis, axis=dim, tiled=True)  18.9 us
    dot_general x1, matrix products, body(): lax.dot_general(lax.all_gather(out_embed, DP, axis=1, tiled=True), full_h...  18.3 us
    all_to_all x1, blocking collectives, side_by_side(): lax.all_to_all(both, axis, split_axis=split_dim, concat_axis=concat_dim,...  18 us
  transfers between devices with their start and end apart: 2, of which 2 were waited for; matrix products, arithmetic and copies ran while one was open for 0% of the time, Pallas kernels for 0%

commit v1 on v0

v1 whole, which is shorter than its diff:
```python
import functools

import jax
import jax.numpy as jnp
from jax import lax
from jax.experimental import pallas as pl
from jax.experimental.pallas import tpu as pltpu
from jax.sharding import Mesh
from jax.sharding import PartitionSpec as P

NX, NC, NZ, NY = 4, 2, 8, 4
ROWS = 128
PAIR = 2 * ROWS


class Message:
    def __init__(self, link, size, to, copy, deps):
        self.link, self.size, self.to, self.copy, self.deps = link, size, to, copy, deps
        self.index = None


def plan_messages(tokens, depth, vocab, width):
    m = {}
    blocks = vocab // ROWS
    pairs = blocks // 2
    xbytes = ROWS * width * 2
    for j in range(pairs):
        for d in (1, -1):
            order = (2 * j, 2 * j + 1) if d == 1 else (2 * j + 1, 2 * j)
            behind = []
            if j >= 2:
                behind = [("xo", d, 2 * (j - 2) + (1 if d == 1 else 0))]
            for b in order:
                m["xo", d, b] = Message(("x", d), xbytes, {"x": d}, ("own_e", 0, b * ROWS, ROWS), behind)
            b = order[0]
            m["xf", d, b] = Message(("x", d), xbytes, {"x": d}, ("e", -d, b * ROWS, ROWS), [("xo", d, b)])
        both = (2 * j, 2 * j + 1)
        for name, where, deps in (
            ("d1", -1, [("xo", 1, b) for b in both]),
            ("d2", 1, [("xo", -1, b) for b in both]),
            ("d3", 2, [("xf", 1, both[0]), ("xf", -1, both[1])]),
        ):
            m[name, j] = Message(("d",), 2 * xbytes, {"c": 1}, ("e", where, j * PAIR, PAIR), deps)
    m["do",] = Message(("d",), vocab * width * 2, {"c": 1}, ("own_e", 0, 0, vocab), [])

    half, quarter = tokens // 2, tokens // 4
    hbytes = half * depth * 2
    for d in (1, -1):
        for s in range(1, 5):
            at, n = (0, half) if s < 4 else ((0, quarter) if d == 1 else (quarter, quarter))
            kind = "own_h" if s == 1 else "h"
            deps = [] if s == 1 else [("az", d, s - 1)]
            m["az", d, s] = Message(("z", d), n * depth * 2, {"z": d}, (kind, (-d * (s - 1), 0), at, n), deps)
    for dz in range(-3, 5):
        if dz == 0:
            deps = []
        elif dz == 4:
            deps = [("az", 1, 4), ("az", -1, 4)]
        else:
            deps = [("az", 1, -dz)] if dz < 0 else [("az", -1, dz)]
        for d in (1, -1):
            m["ay", d, dz] = Message(("y", d), hbytes, {"y": d}, ("own_h" if dz == 0 else "h", (dz, 0), 0, half), deps)
        d = 1 if dz % 2 == 0 else -1
        m["ayf", d, dz] = Message(("y", d), hbytes, {"y": d}, ("h", (dz, -d), 0, half), [("ay", d, dz)])
    for d in (1, -1):
        m["by", d] = Message(("y", d), hbytes, {"y": d}, ("own_h", (0, 0), half, half), [])
        at = half if d == 1 else half + quarter
        m["byf", d] = Message(("y", d), hbytes // 2, {"y": d}, ("h", (0, -d), at, quarter), [("by", d)])
    for dy in (0, 1, -1, 2):
        first = {0: [], 1: [("by", -1)], -1: [("by", 1)], 2: [("byf", 1), ("byf", -1)]}[dy]
        for d in (1, -1):
            for s in range(1, 5):
                at, n = (half, half) if s < 4 else ((half, quarter) if d == 1 else (half + quarter, quarter))
                kind = "own_h" if s == 1 and dy == 0 else "h"
                deps = first if s == 1 else [("bz", d, dy, s - 1)]
                m["bz", d, dy, s] = Message(("z", d), n * depth * 2, {"z": d}, (kind, (-d * (s - 1), dy), at, n), deps)
    for i, one in enumerate(m.values()):
        one.index = i
    return m


def arrivals(m):
    rate = {"x": 46.0e3, "y": 46.0e3, "z": 46.0e3, "d": 500.0e3}
    free, when, left = {}, {}, dict(m)

    def send(name, now):
        one = m[name]
        begin = max(now, free.get(one.link, 0.0))
        free[one.link] = begin + one.size / rate[one.link[0]]
        when[name] = free[one.link] + (1.0 if one.link[0] == "d" else 2.0)
        del left[name]

    initial = [n for n in m if not m[n].deps]
    for n in initial:
        send(n, 0.0)
    order, done = [], set()
    while len(done) < len(m):
        n = min((k for k in when if k not in done), key=lambda k: (when[k], m[k].index))
        done.add(n)
        released = [k for k in left if all(q in done for q in m[k].deps)]
        for k in released:
            send(k, when[n])
        order.append((n, when[n], released))
    return initial, order


def program_order(m, pairs, step_us):
    initial, order = arrivals(m)
    hidden = {n for n in m if n[0] in ("az", "ay", "ayf", "by", "byf", "bz")}

    def needs(j):
        names = {("do",), ("d1", j), ("d2", j), ("d3", j)}
        for b in (2 * j, 2 * j + 1):
            names |= {("xo", 1, b), ("xo", -1, b)}
        names |= {("xf", 1, 2 * j), ("xf", -1, 2 * j + 1)}
        return names | hidden

    def early(j):
        return needs(j) - {("d3", j), ("xf", 1, 2 * j), ("xf", -1, 2 * j + 1)}

    out, waited, clock, i, j, part = [("send", initial)], set(), 0.0, 0, 0, 0
    while i < len(order) or j < pairs:
        idle = i == len(order) or order[i][1] > clock
        last = j == pairs - 1
        if j < pairs and idle and part == 0 and needs(j) <= waited:
            out.append(("matmul", j, 0, 4))
            clock += step_us
            j += 1
        elif last and idle and part == 0 and early(j) <= waited:
            out.append(("matmul", j, 0, 3))
            clock += step_us * 0.75
            part = 1
        elif last and idle and part == 1 and needs(j) <= waited:
            out.append(("matmul", j, 3, 4))
            j += 1
        else:
            n, t, released = order[i]
            clock = max(clock, t)
            out.append(("wait", n))
            waited.add(n)
            if released:
                out.append(("send", released))
            i += 1
    return out


def kernel(m, steps, total_tokens, hid, emb, lab, out, e, h, acc, top, mass, mark, sz, sy, sx, rows, sent, came, own, tail_sent, tail_came):
    x, c = lax.axis_index("x"), lax.axis_index("c")
    z, y = lax.axis_index("z"), lax.axis_index("y")
    size = {"x": NX, "c": NC, "z": NZ, "y": NY}
    pos = {"x": x, "c": c, "z": z, "y": y}
    tokens = lab.shape[1]
    vocab = emb.shape[0]

    def shifted(axis, d):
        return lax.rem(pos[axis] + (d + size[axis]), size[axis])

    def device(to):
        return {axis: shifted(axis, d) for axis, d in to.items()}

    barrier = pltpu.get_barrier_semaphore()
    peers = [{"z": d} for d in range(1, NZ)] + [{"y": d} for d in range(1, NY)]
    others = [{"x": dx, "c": dc} for dx in range(NX) for dc in range(NC) if dx or dc]
    for to in peers + others:
        pl.semaphore_signal(barrier, inc=1, device_id=device(to), device_id_type=pl.DeviceIdType.MESH)
    pl.semaphore_wait(barrier, len(peers) + len(others))

    def chunk_e(dx):
        return shifted("x", dx) * NC + c

    def chunk_h(dz, dy):
        return shifted("z", dz) * NY + shifted("y", dy)

    def descriptor(one):
        kind, where, at, n = one.copy
        part = pl.ds(at, n)
        if kind in ("own_e", "e"):
            dst = e.at[chunk_e(where), part]
            src = emb.at[part] if kind == "own_e" else dst
        else:
            dst = h.at[chunk_h(*where), part]
            src = hid.at[part] if kind == "own_h" else dst
        return pltpu.make_async_remote_copy(
            src_ref=src,
            dst_ref=dst,
            send_sem=sent.at[one.index],
            recv_sem=came.at[one.index],
            device_id=device(one.to),
            device_id_type=pl.DeviceIdType.MESH,
        )

    own_h = pltpu.make_async_copy(hid, h.at[chunk_h(0, 0)], own.at[0])
    own_e = pltpu.make_async_copy(emb, e.at[chunk_e(0)], own.at[1])

    top[...] = jnp.full_like(top, -1e30)
    mass[...] = jnp.zeros_like(mass)
    mark[...] = jnp.zeros_like(mark)

    first_row = (z * NY + y) * vocab

    def matmul(j, begin, end):
        part = pl.ds(j * PAIR, PAIR)

        def product(dx):
            at = lax.rem(x + dx, NX)
            left = jnp.concatenate([e[at * NC + i, part] for i in range(NC)], axis=1)
            each = left.shape[1] // hid.shape[1]
            right = jnp.concatenate([h[at * each + i] for i in range(each)], axis=1)
            return lax.dot_general(left, right, (((1,), (1,)), ((), ())), preferred_element_type=jnp.float32)

        if begin == 0:
            acc[...] = product(0)
            begin = 1

        def more(q, carry):
            acc[...] += product(lax.rem(q + 1, 3) + 1)
            return carry

        lax.fori_loop(begin, end, more, 0)

    def absorb(j):
        def lanes(t, carry):
            at = pl.ds(pl.multiple_of(t * 128, 128), 128)
            block = acc[:, at].reshape(PAIR // 8, 8, 128)
            before = top[:, at]
            peak = jnp.maximum(before, jnp.max(block, axis=0))
            mass[:, at] = mass[:, at] * jnp.exp(before - peak) + jnp.sum(jnp.exp(block - peak[None]), axis=0)
            top[:, at] = peak
            row = lax.broadcasted_iota(jnp.int32, block.shape, 0) * 8 + lax.broadcasted_iota(jnp.int32, block.shape, 1)
            wanted = jnp.broadcast_to(lab[:, at] - (first_row + j * PAIR), (8, 128))
            mark[:, at] += jnp.sum(jnp.where(row == wanted[None], block, 0.0), axis=0)
            return carry

        lax.fori_loop(0, tokens // 128, lanes, 0)

    started = False
    for step in steps:
        if step[0] == "send":
            for name in step[1]:
                descriptor(m[name]).start()
            if not started:
                own_h.start()
                own_e.start()
                started = True
        elif step[0] == "wait":
            descriptor(m[step[1]]).wait_recv()
        else:
            _, j, begin, end = step
            if j == 0:
                own_h.wait()
                own_e.wait()
            matmul(j, begin, end)
            if end == 4:
                absorb(j)

    peak = jnp.max(top[...], axis=0, keepdims=True)
    lse = peak + jnp.log(jnp.sum(mass[...] * jnp.exp(top[...] - peak), axis=0, keepdims=True))
    picked = jnp.sum(mark[...], axis=0, keepdims=True)
    sz[z] = jnp.zeros((16, 128), jnp.float32)
    for t in range(tokens // 128):
        sz[z, t : t + 1] = lse[:, t * 128 : (t + 1) * 128]
        sz[z, 8 + t : 9 + t] = picked[:, t * 128 : (t + 1) * 128]

    def exchange(buffer, at, targets, base):
        copies = [
            pltpu.make_async_remote_copy(
                src_ref=buffer.at[at],
                dst_ref=buffer.at[at],
                send_sem=tail_sent.at[base + i],
                recv_sem=tail_came.at[base + i],
                device_id=device(to),
                device_id_type=pl.DeviceIdType.MESH,
            )
            for i, to in enumerate(targets)
        ]
        for one in copies:
            one.start()
        for one in copies:
            one.wait_recv()
        return copies

    def joined(stats):
        lse, picked = stats[:, 0:8], stats[:, 8:16]
        peak = jnp.max(lse, axis=0)
        return peak + jnp.log(jnp.sum(jnp.exp(lse - peak[None]), axis=0)), jnp.sum(picked, axis=0)

    pending = exchange(sz, z, [{"z": d} for d in range(1, NZ)], 0)
    lse, picked = joined(sz[...])
    sy[y, 0:8] = lse
    sy[y, 8:16] = picked
    pending += exchange(sy, y, [{"y": d} for d in range(1, NY)], NZ - 1)
    lse, picked = joined(sy[...])
    real = lax.broadcasted_iota(jnp.int32, (8, 128), 0) < tokens // 128
    loss = jnp.where(real, lse - picked, 0.0)
    rows[...] = loss
    me = x * NC + c
    sx[me] = jnp.broadcast_to(jnp.sum(jnp.sum(loss, axis=0, keepdims=True), axis=1, keepdims=True), (8, 128))
    pending += exchange(sx, me, others, NZ - 1 + NY - 1)
    out[8:16] = jnp.sum(sx[...], axis=0) / total_tokens
    share = tokens // (NZ * NY)
    first = (z * NY + y) * share
    line, lane = first // 128, lax.rem(first, 128)
    two = jnp.concatenate([rows[pl.ds(line, 1)], rows[pl.ds(line + 1, 1)]], axis=1)
    two = jnp.broadcast_to(two, (8, 256))
    out[0:8] = pltpu.roll(two, lax.rem(256 - lane, 256), 1)[:, 0:128]

    for one in m.values():
        descriptor(one).wait_send()
    for one in pending:
        one.wait_send()


def body(hidden, out_embed, labels):
    tokens, depth = hidden.shape
    vocab, width = out_embed.shape
    m = plan_messages(tokens, depth, vocab, width)
    steps = program_order(m, vocab // PAIR, 2.5)
    total_tokens = tokens * NX * NC
    n_tail = NZ - 1 + NY - 1 + NX * NC - 1
    f32 = jnp.float32
    out = pl.pallas_call(
        functools.partial(kernel, m, steps, total_tokens),
        out_shape=jax.ShapeDtypeStruct((16, 128), f32),
        in_specs=[
            pl.BlockSpec(memory_space=pl.ANY),
            pl.BlockSpec(memory_space=pl.ANY),
            pl.BlockSpec(memory_space=pltpu.VMEM),
        ],
        out_specs=pl.BlockSpec(memory_space=pltpu.VMEM),
        scratch_shapes=[
            pltpu.VMEM((NX * NC, vocab, width), jnp.bfloat16),
            pltpu.VMEM((NZ * NY, tokens, depth), jnp.bfloat16),
            pltpu.VMEM((PAIR, tokens), f32),
            pltpu.VMEM((8, tokens), f32),
            pltpu.VMEM((8, tokens), f32),
            pltpu.VMEM((8, tokens), f32),
            pltpu.VMEM((NZ, 16, 128), f32),
            pltpu.VMEM((NY, 16, 128), f32),
            pltpu.VMEM((NX * NC, 8, 128), f32),
            pltpu.VMEM((8, 128), f32),
            pltpu.SemaphoreType.DMA((len(m),)),
            pltpu.SemaphoreType.DMA((len(m),)),
            pltpu.SemaphoreType.DMA((2,)),
            pltpu.SemaphoreType.DMA((n_tail,)),
            pltpu.SemaphoreType.DMA((n_tail,)),
        ],
        compiler_params=pltpu.CompilerParams(
            collective_id=0, has_side_effects=True, vmem_limit_bytes=60 * 1024 * 1024
        ),
    )(hidden, out_embed, labels.reshape(1, tokens))
    return out[0, : tokens // (NZ * NY)], out[8, 0]


def solution(mesh):
    finer = Mesh(mesh.devices.reshape(NX, NC, NZ, NY), ("x", "c", "z", "y"))
    dp, tensor = ("x", "c"), ("z", "y")
    return jax.shard_map(
        body,
        mesh=finer,
        in_specs=(P(dp, tensor), P(tensor, dp), P(dp)),
        out_specs=(P(dp + tensor), P()),
        check_vma=False,
    )
```

time: 282 us -> 105 us (0.37); the launches traced: 278 us -> 105 us
  waiting for transfers between devices: 165 us -> 0 us
  Pallas kernels: 0 us -> 100 us
  blocking collectives: 70.2 us -> 0 us
  matrix products: 18.3 us -> 0 us
  between operations: 16 us -> 0.64 us
  other arithmetic: 5.37 us -> 0 us
    all_gather x2 -> x0, waiting for transfers between devices: 164 us -> none  [the longest x1 88.5 us: body(): lax.all_gather(out_embed, DP, axis=1, tiled=True)]
    pallas_call x0 -> x1, Pallas kernels: none -> 100 us  [body(): pl.pallas_call(functools.partial(kernel, m, steps, total_tokens), out_sha...]
    psum x4 -> x0, blocking collectives: 33.3 us -> none  [one_axis_at_a_time(): shard = lax.psum(shard, axis)]
    all_gather x1 -> x0, blocking collectives: 18.9 us -> none  [whole_of(): shard = lax.all_gather(shard, axis, axis=dim, tiled=True)]
    dot_general x1 -> x0, matrix products: 18.3 us -> none  [body(): lax.dot_general(lax.all_gather(out_embed, DP, axis=1, tiled=True), full_h...]
    all_to_all x1 -> x0, blocking collectives: 18 us -> none  [side_by_side(): lax.all_to_all(both, axis, split_axis=split_dim, concat_axis=concat_dim,...]
    reduce_sum x3 -> x0, other arithmetic: 4.89 us -> none  [the longest x1 3.68 us: block_stats(): exp_total = jnp.sum(jnp.exp(logits - peak_value[None, :]), axis=0)]
  transfers between devices with their start and end apart: 2 -> 0, of which waited for: 2 -> 0; matrix products, arithmetic and copies ran while one was open for 0% -> 0% of each run, Pallas kernels for 0% -> 0%
where the time goes in v1:
time: 105 us
  Pallas kernels  100 us (95%)
  local copies, waits for them, and re-layouts  3.66 us (3%)
    pallas_call x1, Pallas kernels, body(): pl.pallas_call(functools.partial(kernel, m, steps, total_tokens), out_sha...  100 us

profile of v1, /device:TPU:1, one launch (start us, length us, event | category | flops | bytes accessed | tf_op | source)
XLA Modules:
  0.0 104.8 jit_solution(12497497287867229566)
XLA Ops:
  0.6 1.3 %reshape.7.lab = s32[1,768]{1,0:T(1,128)} reshape(s32[768]{0:T(1024)} %param.5) | data formatting | bytes 6144 | tf_op jit(solution)/shard_map/reshape | solution.py:350
  1.9 100.5 %shard_map.50 = f32[16,128]{1,0:T(8,128)} custom-call(bf16[768,128]{1,0:T(8,128)(2,1)} %hid.1, bf16[2048,512]{1,0:T(8,128)(2,1)} %emb.1, s32[1,768]{1,0:T(1,128)} %reshape.7.lab), custom_call_target="tpu_custom_call" | custom-call | tf_op jit(solution)/shard_map/pallas_call | solution.py:321
  102.4 1.2 %slice.7 = f32[1,1]{1,0:T(1,128)} slice(f32[16,128]{1,0:T(8,128)} %shard_map.50), slice={[8:9], [0:1]} | slice | bytes 8 | tf_op jit(solution)/shard_map/slice | solution.py:351
  103.6 1.2 %slice_bitcast_fusion = f32[24]{0:T(128)} fusion(f32[16,128]{1,0:T(8,128)} %shard_map.50), kind=kLoop, calls=%fused_computation | loop fusion | bytes 192 | tf_op jit(solution)/shard_map/squeeze | solution.py:351

commit v2 on v0

v2 whole, which is shorter than its diff:
```python
import functools

import jax
import jax.numpy as jnp
from jax import lax
from jax.experimental import pallas as pl
from jax.experimental.pallas import tpu as pltpu
from jax.sharding import Mesh
from jax.sharding import PartitionSpec as P

NX, NC, NZ, NY = 4, 2, 8, 4
STEPS = (256,) * 7 + (192, 64)
TASKS = (
    ((0, 1), 0, 4),
    ((2, 3), 0, 4),
    ((4, 5), 0, 3),
    ((4,), 3, 4),
    ((5,), 3, 4),
    ((6,), 0, 3),
    ((7, 8), 0, 3),
    ((6,), 3, 4),
    ((7,), 3, 4),
    ((8,), 3, 4),
)
AHEAD, SPREAD = 2, 5
Z_FIRST = 448


class Message:
    def __init__(self, event, link, to, what, where, at, n, deps):
        self.event, self.link, self.to, self.deps = event, link, to, deps
        self.what, self.where, self.at, self.n = what, where, at, n


def plan_messages(tokens, depth, vocab, width):
    m = []
    early, late = {}, {}
    for i, (group, begin, end) in enumerate(TASKS):
        for j in group:
            if begin == 0:
                early[j] = i
            if end == 4:
                late[j] = i
    at = 0
    for j, step in enumerate(STEPS):
        n = step // 2
        behind = [("xo", min(j - AHEAD, SPREAD), 1)] if j >= AHEAD else []
        for d in (1, -1):
            mine, other = (at, at + n) if d == 1 else (at + n, at)
            m.append(Message(("xo", j, 0), ("x", d), {"x": d}, "e", 0, mine, n, behind))
            m.append(Message(("xo", j, 1), ("x", d), {"x": d}, "e", 0, other, n, behind))
            m.append(Message(("xf", j), ("x", d), {"x": d}, "e", -d, mine, n, [("xo", j, 0)]))
        for where in (-1, 1):
            m.append(Message(("d", early[j]), ("d",), {"c": 1}, "e", where, at, step, [("xo", j, 0), ("xo", j, 1)]))
        m.append(Message(("d", late[j]), ("d",), {"c": 1}, "e", 2, at, step, [("xf", j)]))
        at += step
    m.append(Message(("do",), ("d",), {"c": 1}, "e", 0, 0, vocab, [("xo", 1, 0)]))

    n = tokens - Z_FIRST
    for d in (1, -1):
        m.append(Message(("by",), ("y", d), {"y": d}, "h", (0, 0), Z_FIRST, n, []))
        at = Z_FIRST if d == 1 else Z_FIRST + n // 2
        m.append(Message(("byf",), ("y", d), {"y": d}, "h", (0, -d), at, n // 2, [("by",)]))

    def along_z(name, dy, at, n, first):
        for d in (1, -1):
            for s in range(1, 5):
                deps = first if s == 1 else [(name, dy, s - 1)]
                here, count = (at, n) if s < 4 else ((at, n // 2) if d == 1 else (at + n // 2, n // 2))
                m.append(Message((name, dy, s), ("z", d), {"z": d}, "h", (-d * (s - 1), dy), here, count, deps))

    along_z("az", 0, 0, Z_FIRST, [])
    for dz in (0, 1, -1, 2, -2, 3, -3, 4):
        deps = [("az", 0, abs(dz))] if dz else []
        for d in (1, -1):
            m.append(Message(("ay", dz), ("y", d), {"y": d}, "h", (dz, 0), 0, Z_FIRST, deps))
        d = 1 if dz % 2 == 0 else -1
        m.append(Message(("ayf", dz), ("y", d), {"y": d}, "h", (dz, -d), 0, Z_FIRST, [("ay", dz)]))
    for dy in (0, 1, -1, 2):
        along_z("bz", dy, Z_FIRST, tokens - Z_FIRST, {0: [], 1: [("by",)], -1: [("by",)], 2: [("byf",)]}[dy])
    for one in m:
        one.size = one.n * 2 * (width if one.what == "e" else depth)
    return m


def arrivals(m):
    rate = {"x": 46.5e3, "y": 46.5e3, "z": 46.5e3, "d": 500.0e3}
    free, when, left, count = {}, {}, list(m), {}
    for one in m:
        count[one.event] = count.get(one.event, 0) + 1

    def send(one, now):
        begin = max(now, free.get(one.link, 0.0))
        free[one.link] = begin + one.size / rate[one.link[0]]
        there = free[one.link] + (1.0 if one.link[0] == "d" else 2.0)
        when[one.event] = max(when.get(one.event, 0.0), there)
        count[one.event] -= 1

    initial = [one for one in m if not one.deps]
    for one in initial:
        send(one, 0.0)
    left = [one for one in m if one.deps]
    order, done = [], set()
    while any(k not in done for k in count):
        k = min((k for k in when if k not in done and not count[k]), key=lambda k: when[k])
        done.add(k)
        released = [one for one in left if done.issuperset(one.deps)]
        left = [one for one in left if one not in released]
        for one in released:
            send(one, when[k])
        order.append((k, when[k], released))
    return initial, order


def program_order(m, step_us):
    initial, order = arrivals(m)
    hidden = {one.event for one in m if one.what == "h"}

    def needs(i, task):
        group, begin, end = task
        names = {("d", i)}
        if begin == 0:
            names |= {("do",)} | {("xo", j, k) for j in group for k in (0, 1)}
        if end == 4:
            names |= {("xf", j) for j in group}
        return names | hidden

    todo = [(needs(i, task), task) for i, task in enumerate(TASKS)]
    out, waited, clock, i = [("send", initial)], set(), 0.0, 0
    while i < len(order) or todo:
        idle = i == len(order) or order[i][1] > clock
        if todo and idle and todo[0][0] <= waited:
            task = todo.pop(0)[1]
            out.append(("matmul", task))
            clock += step_us * sum(STEPS[j] for j in task[0]) * (task[2] - task[1]) / 1024
        else:
            k, t, released = order[i]
            clock = max(clock, t)
            out.append(("wait", k))
            waited.add(k)
            if released:
                out.append(("send", released))
            i += 1
    return out


def kernel(m, steps, hid, emb, lab, token_loss, mean_loss, e, h, acc, top, mass, mark, sz, s2, sl, rows, came, sent, own, tail_sent, tail_came):
    x, c = lax.axis_index("x"), lax.axis_index("c")
    z, y = lax.axis_index("z"), lax.axis_index("y")
    size = {"x": NX, "c": NC, "z": NZ, "y": NY}
    pos = {"x": x, "c": c, "z": z, "y": y}
    lines = lab.shape[0]
    tokens = lines * 128
    vocab = emb.shape[0]

    def shifted(axis, d):
        return lax.rem(pos[axis] + (d + size[axis]), size[axis])

    def device(to):
        return {axis: shifted(axis, d) for axis, d in to.items()}

    def chunk_e(dx):
        return shifted("x", dx) * NC + c

    def chunk_h(dz, dy):
        return shifted("z", dz) * NY + shifted("y", dy)

    own_e = pltpu.make_async_copy(emb, e.at[chunk_e(0)], own.at[0])
    own_h = pltpu.make_async_copy(hid, h.at[chunk_h(0, 0)], own.at[1])
    own_e.start()
    own_h.start()

    barrier = pltpu.get_barrier_semaphore()
    near = [{"x": 1}, {"x": -1}, {"c": 1}, {"z": 1}, {"z": -1}, {"y": 1}, {"y": -1}]
    for to in near:
        pl.semaphore_signal(barrier, inc=1, device_id=device(to), device_id_type=pl.DeviceIdType.MESH)
    top[...] = jnp.full_like(top, -1e30)
    mass[...] = jnp.zeros_like(mass)
    mark[...] = jnp.zeros_like(mark)
    own_e.wait()
    own_h.wait()
    pl.semaphore_wait(barrier, len(near))

    events = {}
    for one in m:
        events.setdefault(one.event, []).append(one)
    number = {event: i for i, event in enumerate(events)}

    def copy(src, dst, send_sem, recv_sem, to):
        return pltpu.make_async_remote_copy(
            src_ref=src,
            dst_ref=dst,
            send_sem=send_sem,
            recv_sem=recv_sem,
            device_id=device(to),
            device_id_type=pl.DeviceIdType.MESH,
        )

    def start_message(one):
        part = pl.ds(one.at, one.n)
        ref = e.at[chunk_e(one.where), part] if one.what == "e" else h.at[chunk_h(*one.where), part]
        copy(ref, ref, sent.at[0 if one.what == "e" else 1], came.at[number[one.event]], one.to).start()

    def wait_event(event):
        some = events[event]
        ref = e if some[0].what == "e" else h
        total = sum(one.n for one in some)
        chunks = next(k for k in range(1, 9) if total % k == 0 and total // k <= ref.shape[1])
        ref = ref.at[pl.ds(0, chunks), pl.ds(0, total // chunks)]
        copy(ref, ref, sent.at[0], came.at[number[event]], some[0].to).wait_recv()

    first_row = (z * NY + y) * vocab

    start = [sum(STEPS[:j]) for j in range(len(STEPS))]

    def matmul(first, n, begin, end):
        part = pl.ds(first, n)

        def product(dx):
            at = lax.rem(x + dx, NX)
            left = jnp.concatenate([e[at * NC + i, part] for i in range(NC)], axis=1)
            each = left.shape[1] // hid.shape[1]
            right = jnp.concatenate([h[at * each + i] for i in range(each)], axis=1)
            return lax.dot_general(left, right, (((1,), (1,)), ((), ())), preferred_element_type=jnp.float32)

        if begin == 0:
            acc[part] = product(0)
            begin = 1

        def more(q, carry):
            acc[part] += product(lax.rem(q + 1, 3) + 1)
            return carry

        lax.fori_loop(begin, end, more, 0)

    def absorb(first, n):
        def lanes(t, carry):
            at = pl.ds(pl.multiple_of(t * 128, 128), 128)
            block = acc[pl.ds(first, n), at].reshape(n // 8, 8, 128)
            before = top[:, at]
            peak = jnp.maximum(before, jnp.max(block, axis=0))
            mass[:, at] = mass[:, at] * jnp.exp(before - peak) + jnp.sum(jnp.exp(block - peak[None]), axis=0)
            top[:, at] = peak
            row = lax.broadcasted_iota(jnp.int32, block.shape, 0) * 8 + lax.broadcasted_iota(jnp.int32, block.shape, 1)
            wanted = jnp.broadcast_to(lab[pl.ds(t, 1)] - (first_row + first), (8, 128))
            mark[:, at] += jnp.sum(jnp.where(row == wanted[None], block, 0.0), axis=0)
            return carry

        lax.fori_loop(0, lines, lanes, 0)

    for step in steps:
        if step[0] == "send":
            for one in step[1]:
                start_message(one)
        elif step[0] == "wait":
            wait_event(step[1])
        else:
            group, begin, end = step[1]
            first, n = start[group[0]], sum(STEPS[j] for j in group)
            matmul(first, n, begin, end)
            if end == 4:
                absorb(first, n)

    peak = jnp.max(top[...], axis=0, keepdims=True)
    lse = peak + jnp.log(jnp.sum(mass[...] * jnp.exp(top[...] - peak), axis=0, keepdims=True))
    picked = jnp.sum(mark[...], axis=0, keepdims=True)
    for t in range(lines):
        sz[z, t : t + 1] = lse[:, t * 128 : (t + 1) * 128]
        sz[z, lines + t : lines + t + 1] = picked[:, t * 128 : (t + 1) * 128]

    def combined(lse, axis):
        peak = jnp.max(lse, axis=axis, keepdims=True)
        return jnp.squeeze(peak, axis) + jnp.log(jnp.sum(jnp.exp(lse - peak), axis=axis))

    def spread(i, buffer, at, targets):
        for to in targets:
            copy(buffer.at[at], buffer.at[at], tail_sent.at[i], tail_came.at[i], to).start()
        all_of_them = buffer.at[pl.ds(0, len(targets))]
        return copy(all_of_them, all_of_them, tail_sent.at[i], tail_came.at[i], targets[0])

    along_z = spread(0, sz, z, [{"z": d} for d in (4, 3, -3, 2, -2, 1, -1)])
    along_z.wait_recv()
    me = (x * NC + c) * NY + y
    picked = jnp.sum(sz[:, lines : 2 * lines], axis=0)
    s2[me, 0:lines] = combined(sz[:, 0:lines], 0)
    s2[me, lines : lines + 1] = jnp.sum(picked, axis=0, keepdims=True)
    sl[y] = picked
    order = (2, 1, -1, 0)
    across = spread(1, s2, me, [{"x": i, "y": j, "c": k} for i in order for j in order for k in (0, 1) if i or j or k])
    along_y = spread(2, sl, y, [{"y": j} for j in (2, 1, -1)])
    across.wait_recv()
    along_y.wait_recv()
    whole = s2[...].reshape(NX * NC, NY, lines + 1, 128)
    each = jnp.sum(combined(whole[:, :, 0:lines], 1), axis=1) - jnp.sum(whole[:, :, lines], axis=1)
    mean_loss[...] = jnp.sum(jnp.sum(each, axis=0, keepdims=True), axis=1, keepdims=True) / (tokens * NX * NC)
    mine = s2[pl.ds((x * NC + c) * NY, NY)]
    rows[0:lines] = combined(mine[:, 0:lines], 0) - jnp.sum(sl[...], axis=0)
    rows[lines : lines + 1] = jnp.zeros((1, 128), jnp.float32)
    share = tokens // (NZ * NY)
    first = (z * NY + y) * share
    line, lane = first // 128, lax.rem(first, 128)
    two = jnp.concatenate([rows[pl.ds(line, 1)], rows[pl.ds(line + 1, 1)]], axis=1)
    two = jnp.broadcast_to(two, (8, 256))
    token_loss[...] = pltpu.roll(two, lax.rem(256 - lane, 256), 1)[0:1, 0:share]

    for i, ref in enumerate((e, h)):
        one = [k for k in m if k.what == "eh"[i]]
        whole = ref.at[pl.ds(0, sum(k.n for k in one) // ref.shape[1])]
        copy(whole, whole, sent.at[i], came.at[0], one[0].to).wait_send()
    for one in (along_z, across, along_y):
        one.wait_send()


def body(hidden, out_embed, labels):
    tokens, depth = hidden.shape
    vocab, width = out_embed.shape
    lines = tokens // 128
    m = plan_messages(tokens, depth, vocab, width)
    steps = program_order(m, 2.4)
    f32 = jnp.float32
    token_loss, mean_loss = pl.pallas_call(
        functools.partial(kernel, m, steps),
        out_shape=(
            jax.ShapeDtypeStruct((1, tokens // (NZ * NY)), f32),
            jax.ShapeDtypeStruct((1, 1), f32),
        ),
        in_specs=[
            pl.BlockSpec(memory_space=pl.ANY),
            pl.BlockSpec(memory_space=pl.ANY),
            pl.BlockSpec(memory_space=pltpu.VMEM),
        ],
        out_specs=(pl.BlockSpec(memory_space=pltpu.VMEM), pl.BlockSpec(memory_space=pltpu.VMEM)),
        scratch_shapes=[
            pltpu.VMEM((NX * NC, vocab, width), jnp.bfloat16),
            pltpu.VMEM((NZ * NY, tokens, depth), jnp.bfloat16),
            pltpu.VMEM((vocab, tokens), f32),
            pltpu.VMEM((8, tokens), f32),
            pltpu.VMEM((8, tokens), f32),
            pltpu.VMEM((8, tokens), f32),
            pltpu.VMEM((NZ, 2 * lines, 128), f32),
            pltpu.VMEM((NX * NC * NY, lines + 1, 128), f32),
            pltpu.VMEM((NY, lines, 128), f32),
            pltpu.VMEM((lines + 1, 128), f32),
            pltpu.SemaphoreType.DMA((len({one.event for one in m}),)),
            pltpu.SemaphoreType.DMA((2,)),
            pltpu.SemaphoreType.DMA((2,)),
            pltpu.SemaphoreType.DMA((3,)),
            pltpu.SemaphoreType.DMA((3,)),
        ],
        compiler_params=pltpu.CompilerParams(
            collective_id=0, has_side_effects=True, vmem_limit_bytes=60 * 1024 * 1024
        ),
    )(hidden, out_embed, labels.reshape(lines, 128))
    return token_loss.reshape(-1), mean_loss.reshape(())


def solution(mesh):
    finer = Mesh(mesh.devices.reshape(NX, NC, NZ, NY), ("x", "c", "z", "y"))
    dp, tensor = ("x", "c"), ("z", "y")
    return jax.shard_map(
        body,
        mesh=finer,
        in_specs=(P(dp, tensor), P(tensor, dp), P(dp)),
        out_specs=(P(dp + tensor), P()),
        check_vma=False,
    )
```

time: 282 us -> 97.8 us (0.35); the launches traced: 278 us -> 97.7 us
  waiting for transfers between devices: 165 us -> 0 us
  Pallas kernels: 0 us -> 94.1 us
  blocking collectives: 70.2 us -> 0 us
  matrix products: 18.3 us -> 0 us
  between operations: 16 us -> 2.4 us
  other arithmetic: 5.37 us -> 0 us
    all_gather x2 -> x0, waiting for transfers between devices: 164 us -> none  [the longest x1 88.5 us: body(): lax.all_gather(out_embed, DP, axis=1, tiled=True)]
    pallas_call x0 -> x1, Pallas kernels: none -> 94.1 us  [body(): pl.pallas_call(functools.partial(kernel, m, steps), out_shape=(jax.ShapeD...]
    psum x4 -> x0, blocking collectives: 33.3 us -> none  [one_axis_at_a_time(): shard = lax.psum(shard, axis)]
    all_gather x1 -> x0, blocking collectives: 18.9 us -> none  [whole_of(): shard = lax.all_gather(shard, axis, axis=dim, tiled=True)]
    dot_general x1 -> x0, matrix products: 18.3 us -> none  [body(): lax.dot_general(lax.all_gather(out_embed, DP, axis=1, tiled=True), full_h...]
    all_to_all x1 -> x0, blocking collectives: 18 us -> none  [side_by_side(): lax.all_to_all(both, axis, split_axis=split_dim, concat_axis=concat_dim,...]
    reduce_sum x3 -> x0, other arithmetic: 4.89 us -> none  [the longest x1 3.68 us: block_stats(): exp_total = jnp.sum(jnp.exp(logits - peak_value[None, :]), axis=0)]
  transfers between devices with their start and end apart: 2 -> 0, of which waited for: 2 -> 0; matrix products, arithmetic and copies ran while one was open for 0% -> 0% of each run, Pallas kernels for 0% -> 0%
where the time goes in v2:
time: 97.8 us; the launch traced here: 97.7 us
  Pallas kernels  94.1 us (96%)
  between operations  2.4 us (2%)
  local copies, waits for them, and re-layouts  1.11 us (1%)
    pallas_call x1, Pallas kernels, body(): pl.pallas_call(functools.partial(kernel, m, steps), out_shape=(jax.ShapeD...  94.1 us

profile of v2, /device:TPU:1, one launch (start us, length us, event | category | flops | bytes accessed | tf_op | source)
XLA Modules:
  0.0 97.7 jit_solution(14389868003433417581)
XLA Ops:
  0.6 94.1 %shard_map.50 = (f32[1,24]{1,0:T(1,128)}, f32[1,1]{1,0:T(1,128)}) custom-call(bf16[768,128]{1,0:T(8,128)(2,1)} %hid.1, bf16[2048,512]{1,0:T(8,128)(2,1)} %emb.1, s32[6,128]{1,0:T(8,128)} %bitcast.3), custom_call_target="tpu_custom_call" | custom-call | tf_op jit(solution)/shard_map/pallas_call | solution.py:321
  94.8 1.1 %copy.7 = f32[24]{0:T(128)} copy(f32[24]{0:T(128)} %bitcast.4) | data formatting | bytes 192

commit v3 on v2

--- a/solution.py
+++ b/solution.py
@@ -19,8 +19,8 @@
     ((6,), 0, 3),
     ((7, 8), 0, 3),
     ((6,), 3, 4),
-    ((7,), 3, 4),
-    ((8,), 3, 4),
+    ((7, 8), 3, 3.5),
+    ((7, 8), 3.5, 4),
 )
 AHEAD, SPREAD = 2, 5
 Z_FIRST = 448
@@ -118,6 +118,8 @@
 
     def needs(i, task):
         group, begin, end = task
+        if end == 3.5:
+            return {("xf", j) for j in group}
         names = {("d", i)}
         if begin == 0:
             names |= {("do",)} | {("xo", j, k) for j in group for k in (0, 1)}
@@ -144,12 +146,12 @@
     return out
 
 
-def kernel(m, steps, hid, emb, lab, token_loss, mean_loss, e, h, acc, top, mass, mark, sz, s2, sl, rows, came, sent, own, tail_sent, tail_came):
+def kernel(m, steps, hid, emb, lab_hbm, token_loss, mean_loss, lab, e, h, acc, top, mass, mark, sz, s2, lz, ly, rows, came, sent, own, tail_sent, tail_came):
     x, c = lax.axis_index("x"), lax.axis_index("c")
     z, y = lax.axis_index("z"), lax.axis_index("y")
     size = {"x": NX, "c": NC, "z": NZ, "y": NY}
     pos = {"x": x, "c": c, "z": z, "y": y}
-    lines = lab.shape[0]
+    lines = lab_hbm.shape[0]
     tokens = lines * 128
     vocab = emb.shape[0]
 
@@ -165,20 +167,24 @@
     def chunk_h(dz, dy):
         return shifted("z", dz) * NY + shifted("y", dy)
 
-    own_e = pltpu.make_async_copy(emb, e.at[chunk_e(0)], own.at[0])
-    own_h = pltpu.make_async_copy(hid, h.at[chunk_h(0, 0)], own.at[1])
-    own_e.start()
-    own_h.start()
+    first_rows = pl.ds(0, sum(STEPS[:AHEAD]))
+    other_rows = pl.ds(sum(STEPS[:AHEAD]), vocab - sum(STEPS[:AHEAD]))
+    own_first = pltpu.make_async_copy(emb.at[first_rows], e.at[chunk_e(0), first_rows], own.at[0])
+    own_hidden = pltpu.make_async_copy(hid, h.at[chunk_h(0, 0)], own.at[1])
+    own_other = pltpu.make_async_copy(emb.at[other_rows], e.at[chunk_e(0), other_rows], own.at[2])
+    own_labels = pltpu.make_async_copy(lab_hbm, lab, own.at[3])
+    own_first.start()
 
     barrier = pltpu.get_barrier_semaphore()
     near = [{"x": 1}, {"x": -1}, {"c": 1}, {"z": 1}, {"z": -1}, {"y": 1}, {"y": -1}]
     for to in near:
         pl.semaphore_signal(barrier, inc=1, device_id=device(to), device_id_type=pl.DeviceIdType.MESH)
+    for one in (own_hidden, own_other, own_labels):
+        one.start()
     top[...] = jnp.full_like(top, -1e30)
     mass[...] = jnp.zeros_like(mass)
     mark[...] = jnp.zeros_like(mark)
-    own_e.wait()
-    own_h.wait()
+    own_first.wait()
     pl.semaphore_wait(barrier, len(near))
 
     events = {}
@@ -215,6 +221,16 @@
 
     def matmul(first, n, begin, end):
         part = pl.ds(first, n)
+
+        def half(core):
+            at = lax.rem(x + 2, NX) * NC + core
+            each = emb.shape[1] // hid.shape[1]
+            right = jnp.concatenate([h[at * each + i] for i in range(each)], axis=1)
+            return lax.dot_general(e[at, part], right, (((1,), (1,)), ((), ())), preferred_element_type=jnp.float32)
+
+        if begin == 3.5 or end == 3.5:
+            acc[part] += half(c if end == 3.5 else 1 - c)
+            return
 
         def product(dx):
             at = lax.rem(x + dx, NX)
@@ -250,8 +266,19 @@
 
     for step in steps:
         if step[0] == "send":
+            if step[1][0].deps:
+                for one in step[1]:
+                    start_message(one)
+                continue
             for one in step[1]:
-                start_message(one)
+                if one.what == "e":
+                    start_message(one)
+            own_hidden.wait()
+            for one in step[1]:
+                if one.what == "h":
+                    start_message(one)
+            for one in (own_other, own_labels):
+                one.wait()
         elif step[0] == "wait":
             wait_event(step[1])
         else:
@@ -266,7 +293,8 @@
     picked = jnp.sum(mark[...], axis=0, keepdims=True)
     for t in range(lines):
         sz[z, t : t + 1] = lse[:, t * 128 : (t + 1) * 128]
-        sz[z, lines + t : lines + t + 1] = picked[:, t * 128 : (t + 1) * 128]
+        lz[z, t : t + 1] = picked[:, t * 128 : (t + 1) * 128]
+    sz[z, lines : lines + 1] = sum(picked[:, t * 128 : (t + 1) * 128] for t in range(lines))
 
     def combined(lse, axis):
         peak = jnp.max(lse, axis=axis, keepdims=True)
@@ -278,23 +306,25 @@
         all_of_them = buffer.at[pl.ds(0, len(targets))]
         return copy(all_of_them, all_of_them, tail_sent.at[i], tail_came.at[i], targets[0])
 
-    along_z = spread(0, sz, z, [{"z": d} for d in (4, 3, -3, 2, -2, 1, -1)])
+    ring = [{"z": d} for d in (4, 3, -3, 2, -2, 1, -1)]
+    along_z = spread(0, sz, z, ring)
+    labels_z = spread(1, lz, z, ring)
     along_z.wait_recv()
     me = (x * NC + c) * NY + y
-    picked = jnp.sum(sz[:, lines : 2 * lines], axis=0)
     s2[me, 0:lines] = combined(sz[:, 0:lines], 0)
-    s2[me, lines : lines + 1] = jnp.sum(picked, axis=0, keepdims=True)
-    sl[y] = picked
+    s2[me, lines : lines + 1] = jnp.sum(sz[:, lines : lines + 1], axis=0)
     order = (2, 1, -1, 0)
-    across = spread(1, s2, me, [{"x": i, "y": j, "c": k} for i in order for j in order for k in (0, 1) if i or j or k])
-    along_y = spread(2, sl, y, [{"y": j} for j in (2, 1, -1)])
+    across = spread(2, s2, me, [{"x": i, "y": j, "c": k} for i in order for j in order for k in (0, 1) if i or j or k])
+    labels_z.wait_recv()
+    ly[y] = jnp.sum(lz[...], axis=0)
+    labels_y = spread(3, ly, y, [{"y": j} for j in (2, 1, -1)])
+    labels_y.wait_recv()
     across.wait_recv()
-    along_y.wait_recv()
     whole = s2[...].reshape(NX * NC, NY, lines + 1, 128)
     each = jnp.sum(combined(whole[:, :, 0:lines], 1), axis=1) - jnp.sum(whole[:, :, lines], axis=1)
     mean_loss[...] = jnp.sum(jnp.sum(each, axis=0, keepdims=True), axis=1, keepdims=True) / (tokens * NX * NC)
     mine = s2[pl.ds((x * NC + c) * NY, NY)]
-    rows[0:lines] = combined(mine[:, 0:lines], 0) - jnp.sum(sl[...], axis=0)
+    rows[0:lines] = combined(mine[:, 0:lines], 0) - jnp.sum(ly[...], axis=0)
     rows[lines : lines + 1] = jnp.zeros((1, 128), jnp.float32)
     share = tokens // (NZ * NY)
     first = (z * NY + y) * share
@@ -307,7 +337,7 @@
         one = [k for k in m if k.what == "eh"[i]]
         whole = ref.at[pl.ds(0, sum(k.n for k in one) // ref.shape[1])]
         copy(whole, whole, sent.at[i], came.at[0], one[0].to).wait_send()
-    for one in (along_z, across, along_y):
+    for one in (along_z, labels_z, across, labels_y):
         one.wait_send()
 
 
@@ -327,25 +357,27 @@
         in_specs=[
             pl.BlockSpec(memory_space=pl.ANY),
             pl.BlockSpec(memory_space=pl.ANY),
-            pl.BlockSpec(memory_space=pltpu.VMEM),
+            pl.BlockSpec(memory_space=pl.ANY),
         ],
         out_specs=(pl.BlockSpec(memory_space=pltpu.VMEM), pl.BlockSpec(memory_space=pltpu.VMEM)),
         scratch_shapes=[
+            pltpu.VMEM((lines, 128), jnp.int32),
             pltpu.VMEM((NX * NC, vocab, width), jnp.bfloat16),
             pltpu.VMEM((NZ * NY, tokens, depth), jnp.bfloat16),
             pltpu.VMEM((vocab, tokens), f32),
             pltpu.VMEM((8, tokens), f32),
             pltpu.VMEM((8, tokens), f32),
             pltpu.VMEM((8, tokens), f32),
-            pltpu.VMEM((NZ, 2 * lines, 128), f32),
+            pltpu.VMEM((NZ, lines + 1, 128), f32),
             pltpu.VMEM((NX * NC * NY, lines + 1, 128), f32),
+            pltpu.VMEM((NZ, lines, 128), f32),
             pltpu.VMEM((NY, lines, 128), f32),
             pltpu.VMEM((lines + 1, 128), f32),
             pltpu.SemaphoreType.DMA((len({one.event for one in m}),)),
             pltpu.SemaphoreType.DMA((2,)),
-            pltpu.SemaphoreType.DMA((2,)),
-            pltpu.SemaphoreType.DMA((3,)),
-            pltpu.SemaphoreType.DMA((3,)),
+            pltpu.SemaphoreType.DMA((4,)),
+            pltpu.SemaphoreType.DMA((4,)),
+            pltpu.SemaphoreType.DMA((4,)),
         ],
         compiler_params=pltpu.CompilerParams(
             collective_id=0, has_side_effects=True, vmem_limit_bytes=60 * 1024 * 1024

time: 97.8 us -> 96.3 us (0.985)
  Pallas kernels: 94.1 us -> 92.6 us
    pallas_call x1, Pallas kernels: 94.1 us -> 92.6 us  [body(): pl.pallas_call(functools.partial(kernel, m, steps), out_shape=(jax.ShapeD...]
where the time goes in v3:
time: 96.3 us; the launch traced here: 96.1 us
  Pallas kernels  92.6 us (96%)
  between operations  2.4 us (2%)
  local copies, waits for them, and re-layouts  1.11 us (1%)
    pallas_call x1, Pallas kernels, body(): pl.pallas_call(functools.partial(kernel, m, steps), out_shape=(jax.ShapeD...  92.6 us

profile of v3, /device:TPU:1, one launch (start us, length us, event | category | flops | bytes accessed | tf_op | source)
XLA Modules:
  0.0 96.1 jit_solution(2756861129642214236)
XLA Ops:
  0.6 92.6 %shard_map.50 = (f32[1,24]{1,0:T(1,128)}, f32[1,1]{1,0:T(1,128)}) custom-call(bf16[768,128]{1,0:T(8,128)(2,1)} %hid.1, bf16[2048,512]{1,0:T(8,128)(2,1)} %emb.1, s32[6,128]{1,0:T(8,128)} %bitcast.3), custom_call_target="tpu_custom_call" | custom-call | tf_op jit(solution)/shard_map/pallas_call | solution.py:351
  93.2 1.1 %copy.7 = f32[24]{0:T(128)} copy(f32[24]{0:T(128)} %bitcast.4) | data formatting | bytes 192

commit v4 on v2

v4 whole, which is shorter than its diff:
```python
import functools

import jax
import jax.numpy as jnp
from jax import lax
from jax.experimental import pallas as pl
from jax.experimental.pallas import tpu as pltpu
from jax.sharding import Mesh
from jax.sharding import PartitionSpec as P

NX, NC, NZ, NY = 4, 2, 8, 4
BLOCKS = 4
OWN_Z, PART_Z = 480, 320
VIA_P = 192
TILE = 512
SLOW = {
    "o": {
        ("bz", 0): [("az", "o", 0, 2)],
        ("bz", 1): [("az", "o", 0, 2)],
        ("bz", 2): [("az", "o", 0, 1)],
    },
    "p": {
        "az": [("az", "o", 0, 4)],
        "ay": [("ay", "o", 4)],
        ("bz", 0): [("bz", "o", 0, 3)],
        ("bz", 1): [("bz", "o", 1, 3)],
        ("bz", -1): [("bz", "o", 2, 4)],
        ("bz", 2): [("bz", "o", 2, 4)],
    },
}
ROLES = ("me", "p", "q", "opp")


class Message:
    def __init__(self, event, link, to, what, where, at, n, deps, group):
        self.event, self.link, self.to, self.deps = event, link, to, deps
        self.what, self.where, self.at, self.n, self.group = what, where, at, n, group


def plan_messages(tokens, depth, vocab, width):
    m = []
    rows = vocab // 2
    step = rows // BLOCKS
    kept = tokens - VIA_P

    def add(event, link, to, what, where, at, n, deps, group):
        m.append(Message(event, link, to, what, where, at, n, deps, group))

    def gather(t, base, n_z, n_y, first, slow, group):
        def send(name, d_axis, d, where, at, n, deps):
            add(name, (d_axis, d), {d_axis: d}, "h", where, at, n, deps, group)

        at_y = base + n_z
        for d in (1, -1):
            send(("by", t), "y", d, (0, 0), at_y, n_y, first)
            send(("byf", t), "y", d, (0, -d), at_y if d == 1 else at_y + n_y // 2, n_y // 2, [("by", t)])

        def along_z(name, dy, at, n, before):
            for d in (1, -1):
                for s in range(1, 5):
                    deps = before if s == 1 else [(name, t, dy, s - 1)]
                    here, count = (at, n) if s < 4 else ((at, n // 2) if d == 1 else (at + n // 2, n // 2))
                    send((name, t, dy, s), "z", d, (-d * (s - 1), dy), here, count, deps)

        along_z("az", 0, base, n_z, first + slow.get("az", []))
        for dz in (0, 1, -1, 2, -2, 3, -3, 4):
            deps = [("az", t, 0, abs(dz))] if dz else first + slow.get("ay", [])
            for d in (1, -1):
                send(("ay", t, dz), "y", d, (dz, 0), base, n_z, deps)
            d = 1 if dz % 2 == 0 else -1
            send(("ayf", t, dz), "y", d, (dz, -d), base, n_z, [("ay", t, dz)])
        for dy in (0, 1, -1, 2):
            before = {0: first, 1: [("by", t)], -1: [("by", t)], 2: [("byf", t)]}[dy]
            along_z("bz", dy, at_y, n_y, before + slow.get(("bz", dy), []))

    add(("ph",), ("p",), {"p": 1}, "ht", (0, 0), 0, kept, [], 2)
    add(("lab",), ("p",), {"p": 1}, "lab", 0, 0, 0, [], 3)
    for j in range(BLOCKS):
        add(("e1", j), ("q",), {"q": 1}, "e", "me", j * step, step, [], 0)
        last = [("by", "o"), ("byf", "o")] if j == BLOCKS - 1 else []
        add(("e2", j), ("p",), {"p": 1}, "eo", "me", j * step, step, last, 0)
        add(("e3", j), ("q",), {"q": 1}, "e", "p", j * step, step, [("e2", j)], 0)
        for role, name in (("q", "e1"), ("p", "e2"), ("opp", "e3")):
            add(("d", role), ("d",), {"c": 1}, "e", role, j * step, step, [(name, j)], 0)
    add(("d", "me"), ("d",), {"c": 1}, "e", "me", 0, rows, [("by", "o")], 0)
    gather("o", 0, OWN_Z, tokens - OWN_Z, [], SLOW["o"], 1)
    for dz in (0, 1, -1, 2, -2, 3, -3, 4):
        for dy in (0, 1, -1, 2):
            deps = {0: [], 1: [("by", "o")], -1: [("by", "o")], 2: [("byf", "o")]}[dy] if dz == 0 else [("bz", "o", dy, abs(dz))]
            add(("pp", abs(dz)), ("p",), {"p": 1}, "ht", (dz, dy), kept, VIA_P, deps, 2)
    gather("p", tokens, PART_Z, kept - PART_Z, [("ph",)], SLOW["p"], 2)
    for one in m:
        one.size = one.n * 2 * (width if one.what in ("e", "eo") else depth)
    return m


def arrivals(m):
    rate = {"p": 46.0e3, "q": 46.0e3, "y": 46.0e3, "z": 46.0e3, "d": 500.0e3}
    free, when, count = {}, {}, {}
    for one in m:
        count[one.event] = count.get(one.event, 0) + 1

    def send(one, now):
        begin = max(now, free.get(one.link, 0.0))
        free[one.link] = begin + one.size / rate[one.link[0]]
        there = free[one.link] + (1.0 if one.link[0] == "d" else 2.0)
        when[one.event] = max(when.get(one.event, 0.0), there)
        count[one.event] -= 1

    initial = [one for one in m if not one.deps]
    for one in initial:
        send(one, 0.0)
    left = [one for one in m if one.deps]
    order, done = [], set()
    while any(k not in done for k in count):
        k = min((k for k in when if k not in done and not count[k]), key=lambda k: when[k])
        done.add(k)
        released = [one for one in left if done.issuperset(one.deps)]
        left = [one for one in left if one not in released]
        for one in released:
            send(one, when[k])
        order.append((k, when[k], released))
    return initial, order


def program_order(m):
    initial, order = arrivals(m)
    events = {one.event for one in m}
    embed = {"me": {("d", "me")}}
    for role, name in (("q", "e1"), ("p", "e2"), ("opp", "e3")):
        embed[role] = {("d", role)} | {k for k in events if k[0] == name}
    own = {k for k in events if len(k) > 1 and k[1] == "o"}
    todo = [(own | embed[role] | {("lab",)}, (role, 0), 3.4 if role == "opp" else 2.2) for role in ROLES]
    for d in range(5):
        mine = {("pp", d)}
        for k in events:
            if len(k) > 1 and k[1] == "p" and k[0] != "d" and (abs(k[-1]) if k[0] not in ("by", "byf") else 0) == d:
                mine.add(k)
        if d == 0:
            mine.add(("ph",))
        todo.append((mine, (d, 1), 1.1 if d in (0, 4) else 2.2))
    out, waited, clock, i = [("send", initial)], set(), 0.0, 0
    while i < len(order) or todo:
        idle = i == len(order) or order[i][1] > clock
        if todo and idle and todo[0][0] <= waited:
            _, task, cost = todo.pop(0)
            out.append(("matmul", task))
            clock += cost
        else:
            k, t, released = order[i]
            clock = max(clock, t)
            out.append(("wait", k))
            waited.add(k)
            if released:
                out.append(("send", released))
            i += 1
    return out


def kernel(m, steps, hid, emb, lab_hbm, token_loss, mean_loss, lab, e, eo, h, acc, top, mass, mark, sz, sp, s2, lz, lp, ly, rows, came, sent, own, tail_sent, tail_came):
    x, c = lax.axis_index("x"), lax.axis_index("c")
    z, y = lax.axis_index("z"), lax.axis_index("y")
    size = {"x": NX, "c": NC, "z": NZ, "y": NY}
    pos = {"x": x, "c": c, "z": z, "y": y}
    lines = lab_hbm.shape[0]
    tokens = lines * 128
    vocab = emb.shape[0]
    half = vocab // 2
    sign = 1 - 2 * lax.rem(x, 2)
    chip = {"me": x, "p": x + sign, "q": lax.rem(x - sign + NX, NX), "opp": lax.rem(x + 2, NX)}
    mine = lax.rem((x + 1) // 2, 2) * half
    other = half - mine

    def shifted(axis, d):
        return lax.rem(pos[axis] + (d + size[axis]), size[axis])

    def device(to):
        where = {axis: shifted(axis, d) for axis, d in to.items() if axis not in ("p", "q")}
        for role in ("p", "q"):
            if role in to:
                where["x"] = chip[role]
        return where

    def chunk_e(role):
        return chip[role] * NC + c

    def chunk_h(dz, dy):
        return shifted("z", dz) * NY + shifted("y", dy)

    own_eo = pltpu.make_async_copy(emb.at[pl.ds(pl.multiple_of(other, half), half)], eo, own.at[0])
    own_e = pltpu.make_async_copy(emb.at[pl.ds(pl.multiple_of(mine, half), half)], e.at[chunk_e("me")], own.at[1])
    own_h = pltpu.make_async_copy(hid, h.at[chunk_h(0, 0), pl.ds(0, tokens)], own.at[2])
    own_labels = pltpu.make_async_copy(lab_hbm, lab.at[0], own.at[3])
    loads = (own_h, own_labels, own_e, own_eo)
    own_h.start()

    barrier = pltpu.get_barrier_semaphore()
    near = [{"x": 1}, {"x": -1}, {"c": 1}, {"z": 1}, {"z": -1}, {"y": 1}, {"y": -1}]
    for to in near:
        pl.semaphore_signal(barrier, inc=1, device_id=device(to), device_id_type=pl.DeviceIdType.MESH)
    for one in loads[1:]:
        one.start()
    top[...] = jnp.full_like(top, -1e30)
    mass[...] = jnp.zeros_like(mass)
    mark[...] = jnp.zeros_like(mark)
    for one in loads:
        one.wait()
    pl.semaphore_wait(barrier, len(near))

    events = {}
    for one in m:
        events.setdefault(one.event, []).append(one)
    number = {event: i for i, event in enumerate(events)}

    def copy(src, dst, send_sem, recv_sem, to):
        return pltpu.make_async_remote_copy(
            src_ref=src,
            dst_ref=dst,
            send_sem=send_sem,
            recv_sem=recv_sem,
            device_id=device(to),
            device_id_type=pl.DeviceIdType.MESH,
        )

    def start_message(one):
        part = pl.ds(one.at, one.n)
        if one.what == "e":
            src = dst = e.at[chunk_e(one.where), part]
        elif one.what == "eo":
            src, dst = eo.at[part], e.at[chunk_e("me"), part]
        elif one.what == "h":
            src = dst = h.at[chunk_h(*one.where), part]
        elif one.what == "ht":
            src, dst = h.at[chunk_h(*one.where), part], h.at[chunk_h(*one.where), pl.ds(tokens + one.at, one.n)]
        else:
            src, dst = lab.at[0], lab.at[1]
        copy(src, dst, sent.at[one.group], came.at[number[one.event]], one.to).start()

    def wait_event(event):
        some = events[event]
        if some[0].what == "lab":
            ref = lab.at[1]
        else:
            ref = e if some[0].what in ("e", "eo") else h
            total = sum(one.n for one in some)
            chunks = next(k for k in range(1, 9) if total % (16 * k) == 0 and total // k <= ref.shape[1])
            ref = ref.at[pl.ds(0, chunks), pl.ds(0, total // chunks)]
        copy(ref, ref, sent.at[0], came.at[number[event]], some[0].to).wait_recv()

    first_row = (z * NY + y) * vocab + mine

    def matmul(part, token_set):
        at = pl.ds(token_set * tokens, tokens)
        if part in ROLES:
            chunks = [chip[part] * NC + i for i in range(NC)]
        else:
            chunks = [shifted("z", d) for d in sorted({part, part if part in (0, 4) else -part})]
        each = emb.shape[1] // hid.shape[1]

        def tile(i, carry):
            to = pl.ds(pl.multiple_of(i * TILE, TILE), TILE)
            left = jnp.concatenate([e[f, to] for f in chunks], axis=1)
            right = jnp.concatenate([h[f * each + i, at] for f in chunks for i in range(each)], axis=1)
            acc[to, at] += lax.dot_general(left, right, (((1,), (1,)), ((), ())), preferred_element_type=jnp.float32)
            return carry

        lax.fori_loop(0, half // TILE, tile, 0)

    def absorb(token_set):
        n = 256

        def lanes(t, carry):
            at = pl.ds(pl.multiple_of(token_set * tokens + lax.rem(t, lines) * 128, 128), 128)
            first = pl.multiple_of(t // lines * n, n)
            block = acc[pl.ds(first, n), at].reshape(n // 8, 8, 128)
            before = top[:, at]
            peak = jnp.maximum(before, jnp.max(block, axis=0))
            mass[:, at] = mass[:, at] * jnp.exp(before - peak) + jnp.sum(jnp.exp(block - peak[None]), axis=0)
            top[:, at] = peak
            row = lax.broadcasted_iota(jnp.int32, block.shape, 0) * 8 + lax.broadcasted_iota(jnp.int32, block.shape, 1)
            wanted = jnp.broadcast_to(lab[token_set, pl.ds(lax.rem(t, lines), 1)] - (first_row + first), (8, 128))
            mark[:, at] += jnp.sum(jnp.where(row == wanted[None], block, 0.0), axis=0)
            return carry

        lax.fori_loop(0, lines * (half // n), lanes, 0)

    for step in steps:
        if step[0] == "send":
            for one in step[1]:
                start_message(one)
            if not step[1][0].deps:

                def clear(i, carry):
                    acc[pl.ds(pl.multiple_of(i * 16, 16), 16)] = jnp.zeros((16, 2 * tokens), jnp.float32)
                    return carry

                lax.fori_loop(0, half // 16, clear, 0)
        elif step[0] == "wait":
            wait_event(step[1])
        else:
            matmul(*step[1])
            if step[1][0] in ("opp", 4):
                absorb(step[1][1])

    peak = jnp.max(top[...], axis=0, keepdims=True)
    lse = peak + jnp.log(jnp.sum(mass[...] * jnp.exp(top[...] - peak), axis=0, keepdims=True))
    picked = jnp.sum(mark[...], axis=0, keepdims=True)
    slot = 2 * z
    for token_set, (to_s, to_l) in enumerate(((sz.at[slot], lz.at[slot]), (sp, lp))):
        one = [slice(token_set * tokens + t * 128, token_set * tokens + (t + 1) * 128) for t in range(lines)]
        for t in range(lines):
            to_s[t : t + 1] = lse[:, one[t]]
            to_l[t : t + 1] = picked[:, one[t]]
        to_s[lines : lines + 1] = sum(picked[:, k] for k in one)

    def combined(lse, axis):
        peak = jnp.max(lse, axis=axis, keepdims=True)
        return jnp.squeeze(peak, axis) + jnp.log(jnp.sum(jnp.exp(lse - peak), axis=axis))

    def spread(i, buffer, work):
        for src, at, to in work:
            copy(src, buffer.at[at], tail_sent.at[i], tail_came.at[i], to).start()
        all_of_them = buffer.at[pl.ds(0, len(work))]
        return copy(all_of_them, all_of_them, tail_sent.at[i], tail_came.at[i], work[0][2])

    ring = (4, 3, -3, 2, -2, 1, -1, 0)

    def along(buffer, part):
        return [w for d in ring for w in ((part, slot + 1, {"p": 1, "z": d}), (buffer.at[slot], slot, {"z": d}))][:-1]

    along_z = spread(0, sz, along(sz, sp))
    labels_z = spread(1, lz, along(lz, lp))
    along_z.wait_recv()
    me = (x * NC + c) * NY + y
    s2[me, 0:lines] = combined(sz[:, 0:lines], 0)
    s2[me, lines : lines + 1] = jnp.sum(sz[:, lines : lines + 1], axis=0)
    order = (2, 1, -1, 0)
    across = spread(2, s2, [(s2.at[me], me, {"x": i, "y": j, "c": k}) for i in order for j in order for k in (0, 1) if i or j or k])
    labels_z.wait_recv()
    ly[y] = jnp.sum(lz[...], axis=0)
    labels_y = spread(3, ly, [(ly.at[y], y, {"y": j}) for j in (2, 1, -1)])
    labels_y.wait_recv()
    across.wait_recv()
    whole = s2[...].reshape(NX * NC, NY, lines + 1, 128)
    each = jnp.sum(combined(whole[:, :, 0:lines], 1), axis=1) - jnp.sum(whole[:, :, lines], axis=1)
    mean_loss[...] = jnp.sum(jnp.sum(each, axis=0, keepdims=True), axis=1, keepdims=True) / (tokens * NX * NC)
    group = s2[pl.ds((x * NC + c) * NY, NY)]
    rows[0:lines] = combined(group[:, 0:lines], 0) - jnp.sum(ly[...], axis=0)
    rows[lines : lines + 1] = jnp.zeros((1, 128), jnp.float32)
    share = tokens // (NZ * NY)
    first = (z * NY + y) * share
    line, lane = first // 128, lax.rem(first, 128)
    two = jnp.concatenate([rows[pl.ds(line, 1)], rows[pl.ds(line + 1, 1)]], axis=1)
    two = jnp.broadcast_to(two, (8, 256))
    token_loss[...] = pltpu.roll(two, lax.rem(256 - lane, 256), 1)[0:1, 0:share]

    for group in range(4):
        some = [one for one in m if one.group == group]
        if group == 3:
            ref = lab.at[0]
        else:
            ref, n = (e, half) if group == 0 else (h, tokens)
            ref = ref.at[pl.ds(0, sum(one.n for one in some) // n), pl.ds(0, n)]
        copy(ref, ref, sent.at[group], came.at[0], some[0].to).wait_send()
    for one in (along_z, labels_z, across, labels_y):
        one.wait_send()


def body(hidden, out_embed, labels):
    tokens, depth = hidden.shape
    vocab, width = out_embed.shape
    lines = tokens // 128
    m = plan_messages(tokens, depth, vocab, width)
    steps = program_order(m)
    f32 = jnp.float32
    token_loss, mean_loss = pl.pallas_call(
        functools.partial(kernel, m, steps),
        out_shape=(
            jax.ShapeDtypeStruct((1, tokens // (NZ * NY)), f32),
            jax.ShapeDtypeStruct((1, 1), f32),
        ),
        in_specs=[
            pl.BlockSpec(memory_space=pl.ANY),
            pl.BlockSpec(memory_space=pl.ANY),
            pl.BlockSpec(memory_space=pl.ANY),
        ],
        out_specs=(pl.BlockSpec(memory_space=pltpu.VMEM), pl.BlockSpec(memory_space=pltpu.VMEM)),
        scratch_shapes=[
            pltpu.VMEM((2, lines, 128), jnp.int32),
            pltpu.VMEM((NX * NC, vocab // 2, width), jnp.bfloat16),
            pltpu.VMEM((vocab // 2, width), jnp.bfloat16),
            pltpu.VMEM((NZ * NY, 2 * tokens, depth), jnp.bfloat16),
            pltpu.VMEM((vocab // 2, 2 * tokens), f32),
            pltpu.VMEM((8, 2 * tokens), f32),
            pltpu.VMEM((8, 2 * tokens), f32),
            pltpu.VMEM((8, 2 * tokens), f32),
            pltpu.VMEM((2 * NZ, lines + 1, 128), f32),
            pltpu.VMEM((lines + 1, 128), f32),
            pltpu.VMEM((NX * NC * NY, lines + 1, 128), f32),
            pltpu.VMEM((2 * NZ, lines, 128), f32),
            pltpu.VMEM((lines, 128), f32),
            pltpu.VMEM((NY, lines, 128), f32),
            pltpu.VMEM((lines + 1, 128), f32),
            pltpu.SemaphoreType.DMA((len({one.event for one in m}),)),
            pltpu.SemaphoreType.DMA((4,)),
            pltpu.SemaphoreType.DMA((4,)),
            pltpu.SemaphoreType.DMA((4,)),
            pltpu.SemaphoreType.DMA((4,)),
        ],
        compiler_params=pltpu.CompilerParams(
            collective_id=0, has_side_effects=True, vmem_limit_bytes=60 * 1024 * 1024
        ),
    )(hidden, out_embed, labels.reshape(lines, 128))
    return token_loss.reshape(-1), mean_loss.reshape(())


def solution(mesh):
    finer = Mesh(mesh.devices.reshape(NX, NC, NZ, NY), ("x", "c", "z", "y"))
    dp, tensor = ("x", "c"), ("z", "y")
    return jax.shard_map(
        body,
        mesh=finer,
        in_specs=(P(dp, tensor), P(tensor, dp), P(dp)),
        out_specs=(P(dp + tensor), P()),
        check_vma=False,
    )
```

time: 97.8 us -> 91.8 us (0.939)
  Pallas kernels: 94.1 us -> 88.2 us
    pallas_call x1, Pallas kernels: 94.1 us -> 88.2 us  [body(): pl.pallas_call(functools.partial(kernel, m, steps), out_shape=(jax.ShapeD...]
where the time goes in v4:
time: 91.8 us; the launch traced here: 91.7 us
  Pallas kernels  88.2 us (96%)
  between operations  2.4 us (3%)
  local copies, waits for them, and re-layouts  1.11 us (1%)
    pallas_call x1, Pallas kernels, body(): pl.pallas_call(functools.partial(kernel, m, steps), out_shape=(jax.ShapeD...  88.2 us

profile of v4, /device:TPU:1, one launch (start us, length us, event | category | flops | bytes accessed | tf_op | source)
XLA Modules:
  0.0 91.7 jit_solution(10684447487717846868)
XLA Ops:
  0.6 88.2 %shard_map.50 = (f32[1,24]{1,0:T(1,128)}, f32[1,1]{1,0:T(1,128)}) custom-call(bf16[768,128]{1,0:T(8,128)(2,1)} %hid.1, bf16[2048,512]{1,0:T(8,128)(2,1)} %emb.1, s32[6,128]{1,0:T(8,128)} %bitcast.3), custom_call_target="tpu_custom_call" | custom-call | tf_op jit(solution)/shard_map/pallas_call | solution.py:376
  88.8 1.1 %copy.7 = f32[24]{0:T(128)} copy(f32[24]{0:T(128)} %bitcast.4) | data formatting | bytes 192

commit v5 on v4

--- a/solution.py
+++ b/solution.py
@@ -11,8 +11,10 @@
 NX, NC, NZ, NY = 4, 2, 8, 4
 BLOCKS = 4
 OWN_Z, PART_Z = 480, 320
+SOONER = 2.5
 VIA_P = 192
 TILE = 512
+ABSORB_AT = 7
 SLOW = {
     "o": {
         ("bz", 0): [("az", "o", 0, 2)],
@@ -123,38 +125,57 @@
     return initial, order
 
 
-def program_order(m):
-    initial, order = arrivals(m)
+def tasks(m):
     events = {one.event for one in m}
     embed = {"me": {("d", "me")}}
     for role, name in (("q", "e1"), ("p", "e2"), ("opp", "e3")):
         embed[role] = {("d", role)} | {k for k in events if k[0] == name}
-    own = {k for k in events if len(k) > 1 and k[1] == "o"}
-    todo = [(own | embed[role] | {("lab",)}, (role, 0), 3.4 if role == "opp" else 2.2) for role in ROLES]
+    own = {k for k in events if len(k) > 1 and k[1] == "o"} | {("lab",)}
+    out = [(own | embed[role], (role, 0), 2.1) for role in ROLES]
     for d in range(5):
-        mine = {("pp", d)}
+        mine = {("pp", d)} | ({("ph",)} if d == 0 else set())
         for k in events:
             if len(k) > 1 and k[1] == "p" and k[0] != "d" and (abs(k[-1]) if k[0] not in ("by", "byf") else 0) == d:
                 mine.add(k)
-        if d == 0:
-            mine.add(("ph",))
-        todo.append((mine, (d, 1), 1.1 if d in (0, 4) else 2.2))
-    out, waited, clock, i = [("send", initial)], set(), 0.0, 0
-    while i < len(order) or todo:
-        idle = i == len(order) or order[i][1] > clock
-        if todo and idle and todo[0][0] <= waited:
+        out.append((mine, (d, 1), 1.25 if d in (0, 4) else 2.1))
+    out.insert(ABSORB_AT, (set(), ("absorb", 0), 1.8))
+    out.append((set(), ("absorb", 1), 1.8))
+    return out
+
+
+def program_order(m):
+    initial, order = arrivals(m)
+    when = {k: t - (SOONER if k[0] == "e3" else 0.0) for k, t, _ in order}
+    order.sort(key=lambda entry: when[entry[0]])
+    release = {k: released for k, _, released in order}
+    todo, urgent = tasks(m), [k for k, _, released in order if released]
+    out, waited, clock = [("send", initial)], set(), 0.0
+
+    def wait(k):
+        nonlocal clock
+        clock = max(clock, when[k])
+        out.append(("wait", k))
+        waited.add(k)
+        if release[k]:
+            for dep in [dep for one in release[k] for dep in one.deps]:
+                if dep not in waited:
+                    wait(dep)
+            out.append(("send", release[k]))
+            urgent.remove(k)
+
+    while todo or len(waited) < len(when):
+        needs = todo[0][0] - waited if todo else set(when) - waited
+        ready = max([when[k] for k in needs], default=0.0)
+        if urgent and when[urgent[0]] <= max(clock, ready):
+            wait(urgent[0])
+            continue
+        for k in sorted(needs, key=when.get):
+            wait(k)
+        if todo:
             _, task, cost = todo.pop(0)
             out.append(("matmul", task))
             clock += cost
-        else:
-            k, t, released = order[i]
-            clock = max(clock, t)
-            out.append(("wait", k))
-            waited.add(k)
-            if released:
-                out.append(("send", released))
-            i += 1
-    return out
+    return out, clock
 
 
 def kernel(m, steps, hid, emb, lab_hbm, token_loss, mean_loss, lab, e, eo, h, acc, top, mass, mark, sz, sp, s2, lz, lp, ly, rows, came, sent, own, tail_sent, tail_came):
@@ -298,9 +319,10 @@
         elif step[0] == "wait":
             wait_event(step[1])
         else:
-            matmul(*step[1])
-            if step[1][0] in ("opp", 4):
+            if step[1][0] == "absorb":
                 absorb(step[1][1])
+            else:
+                matmul(*step[1])
 
     peak = jnp.max(top[...], axis=0, keepdims=True)
     lse = peak + jnp.log(jnp.sum(mass[...] * jnp.exp(top[...] - peak), axis=0, keepdims=True))
@@ -371,7 +393,7 @@
     vocab, width = out_embed.shape
     lines = tokens // 128
     m = plan_messages(tokens, depth, vocab, width)
-    steps = program_order(m)
+    steps, _ = program_order(m)
     f32 = jnp.float32
     token_loss, mean_loss = pl.pallas_call(
         functools.partial(kernel, m, steps),

time: 91.8 us -> 90.9 us (level)
  no operation moved by 1% of the time
where the time goes in v5:
time: 90.9 us; the launch traced here: 90.8 us
  Pallas kernels  87.3 us (96%)
  between operations  2.4 us (3%)
  local copies, waits for them, and re-layouts  1.11 us (1%)
    pallas_call x1, Pallas kernels, body(): pl.pallas_call(functools.partial(kernel, m, steps), out_shape=(jax.ShapeD...  87.3 us

profile of v5, /device:TPU:1, one launch (start us, length us, event | category | flops | bytes accessed | tf_op | source)
XLA Modules:
  0.0 90.8 jit_solution(3201800023224333219)
XLA Ops:
  0.6 87.3 %shard_map.50 = (f32[1,24]{1,0:T(1,128)}, f32[1,1]{1,0:T(1,128)}) custom-call(bf16[768,128]{1,0:T(8,128)(2,1)} %hid.1, bf16[2048,512]{1,0:T(8,128)(2,1)} %emb.1, s32[6,128]{1,0:T(8,128)} %bitcast.3), custom_call_target="tpu_custom_call" | custom-call | tf_op jit(solution)/shard_map/pallas_call | solution.py:398
  87.9 1.1 %copy.7 = f32[24]{0:T(128)} copy(f32[24]{0:T(128)} %bitcast.4) | data formatting | bytes 192

commit v6 on v5

--- a/solution.py
+++ b/solution.py
@@ -224,8 +224,8 @@
     top[...] = jnp.full_like(top, -1e30)
     mass[...] = jnp.zeros_like(mass)
     mark[...] = jnp.zeros_like(mark)
-    for one in loads:
-        one.wait()
+    own_h.wait()
+    own_labels.wait()
     pl.semaphore_wait(barrier, len(near))
 
     events = {}
@@ -307,9 +307,16 @@
 
     for step in steps:
         if step[0] == "send":
-            for one in step[1]:
+            first = not step[1][0].deps
+            now = [one for one in step[1] if not first or one.what not in ("e", "eo")]
+            for one in now:
                 start_message(one)
-            if not step[1][0].deps:
+            if first:
+                own_e.wait()
+                own_eo.wait()
+                for one in step[1]:
+                    if one not in now:
+                        start_message(one)
 
                 def clear(i, carry):
                     acc[pl.ds(pl.multiple_of(i * 16, 16), 16)] = jnp.zeros((16, 2 * tokens), jnp.float32)

time: 90.9 us -> 91 us (level)
  no operation moved by 1% of the time
where the time goes in v6:
time: 91 us; the launch traced here: 90.8 us
  Pallas kernels  87.3 us (96%)
  between operations  2.4 us (3%)
  local copies, waits for them, and re-layouts  1.11 us (1%)
    pallas_call x1, Pallas kernels, body(): pl.pallas_call(functools.partial(kernel, m, steps), out_shape=(jax.ShapeD...  87.3 us

profile of v6, /device:TPU:1, one launch (start us, length us, event | category | flops | bytes accessed | tf_op | source)
XLA Modules:
  0.0 90.8 jit_solution(14026628584791800253)
XLA Ops:
  0.6 87.3 %shard_map.50 = (f32[1,24]{1,0:T(1,128)}, f32[1,1]{1,0:T(1,128)}) custom-call(bf16[768,128]{1,0:T(8,128)(2,1)} %hid.1, bf16[2048,512]{1,0:T(8,128)(2,1)} %emb.1, s32[6,128]{1,0:T(8,128)} %bitcast.3), custom_call_target="tpu_custom_call" | custom-call | tf_op jit(solution)/shard_map/pallas_call | solution.py:405
  88.0 1.1 %copy.7 = f32[24]{0:T(128)} copy(f32[24]{0:T(128)} %bitcast.4) | data formatting | bytes 192
